TPU v7x, 512 devices: a whole 4x4x16 slice. The times are simulated.
512 devices in a mesh: grp: 4 (over x), dom: 128 (over z, y, core).
Axes of the slice: x: 4, y: 4, z: 16, core: 2. Of those that a mesh axis runs over, the one named last changes fastest.
Arguments:
- node_state: float32 [65536, 6, 128], P(('grp', 'dom')), may hold values from -6 to 6
- node_dest: int32 [65536], P(('grp', 'dom')), may hold values from 0 to 127, as said below
- seg_nodes: float32 [6, 262144], P(None, ('grp', 'dom')), may hold values from -6 to 6
- seg_conn: int32 [3, 524288], P(None, ('grp', 'dom')), may hold values from 0 to 511
- pair_seg: int32 [512, 4, 32], P(('grp', 'dom')), may hold values from 0 to 7
- pair_slot: int32 [512, 4, 32], P(('grp', 'dom')), may hold values from 0 to 255, as said below
Outputs:
- node_force: float32 [65536, 3, 128], P(('grp', 'dom'))
Inputs may be any that keep to these rules, and one draw needn't show every extreme that they name: `node_dest`: at most 2 blocks of one device name the same contact domain; in every grp row one contact domain receives exactly 2 blocks from every device of that row; every device sends at least one block to the contact domain of its own dom index. `pair_slot`: every entry names a slot d * 2 + k that holds a block: device (r, d) sends more than k blocks to the contact domain.
All inputs are finite; a program needn't handle non-finite values.
Results may differ from a plain program's by a relative error of at most 0.00023.
Values sent between devices are 32-bit elements; how exact they have to be, the bound alone decides.
No kernel may reach another device: no remote copies, remote signals or barrier semaphores. Data moves between devices by JAX's collectives and lax.ppermute only.
A program may use at most 64 MiB of HBM per device.

v0:
```python
import jax
import jax.numpy as jnp
from jax import lax
from jax.sharding import Mesh
from jax.sharding import PartitionSpec as P

SEG_BLK = 128
DOM = ("dom_0", "dom_1", "dom_2")
GRP_DOM = ("grp", "dom_0", "dom_1", "dom_2")
time_step = 0.5
stiffness = 0.5
radius_sq = 0.5


def in_blocks(shard, dim, devices):
    dims = shard.shape
    blocks = shard.reshape(*dims[:dim], devices, dims[dim] // devices, *dims[dim + 1 :])
    return jnp.moveaxis(blocks, dim, 0)


def in_order(blocks, dim):
    blocks = jnp.moveaxis(blocks, 0, dim)
    dims = blocks.shape
    return blocks.reshape(*dims[:dim], dims[dim] * dims[dim + 1], *dims[dim + 2 :])


def moved_by_axis(blocks, axes, turns):
    dims = [lax.axis_size(a) for a in axes]
    blocks = blocks.reshape(*dims, *blocks.shape[1:])
    for k in turns:
        blocks = lax.all_to_all(blocks, axes[k], split_axis=k, concat_axis=k, tiled=True)
    return blocks.reshape(-1, *blocks.shape[len(axes) :])


def two_step_exchange(shard, groups, turns, split_dim, concat_dim):
    devices = lax.axis_size(groups[0]) * lax.axis_size(groups[1])
    blocks = in_blocks(shard, split_dim, devices)
    return in_order(moved_by_axis(blocks, groups, turns), concat_dim)


def seg_geometry(corners):
    corner_a = corners[:, 0]
    corner_b = corners[:, 1]
    corner_c = corners[:, 2]
    edge_one = corner_b[0:3] - corner_a[0:3]
    edge_two = corner_c[0:3] - corner_a[0:3]
    normal = 0.5 * jnp.stack(
        [
            edge_one[1] * edge_two[2] - edge_one[2] * edge_two[1],
            edge_one[2] * edge_two[0] - edge_one[0] * edge_two[2],
            edge_one[0] * edge_two[1] - edge_one[1] * edge_two[0],
        ]
    )
    centre = (corner_a[0:3] + corner_b[0:3] + corner_c[0:3]) / 3.0
    motion = (corner_a[3:6] + corner_b[3:6] + corner_c[3:6]) / 3.0
    return jnp.concatenate([normal, centre, motion], axis=0)


def tile_force(node_rows, geometry):
    clearance = jnp.zeros((geometry.shape[1], node_rows.shape[1]), jnp.float32)
    distance = jnp.zeros((geometry.shape[1], node_rows.shape[1]), jnp.float32)
    for axis_id in range(3):
        offset = node_rows[axis_id][None, :] - geometry[3 + axis_id][:, None]
        drift = node_rows[3 + axis_id][None, :] - geometry[6 + axis_id][:, None]
        clearance = clearance + geometry[axis_id][:, None] * (offset + time_step * drift)
        distance = distance + offset * offset
    pressure = stiffness * jnp.exp(-distance / radius_sq) * jnp.maximum(-clearance, 0.0)
    return jnp.dot(
        geometry[0:3], pressure, precision=lax.Precision.HIGHEST, preferred_element_type=jnp.float32
    )


def place_rows(slot_ids, values, slot_total):
    onehot = (slot_ids[None, :] == jnp.arange(slot_total, dtype=jnp.int32)[:, None]).astype(
        jnp.float32
    )
    flattened = values.reshape(values.shape[0], -1)
    placed = jnp.dot(
        onehot, flattened, precision=lax.Precision.HIGHEST, preferred_element_type=jnp.float32
    )
    return placed.reshape((slot_total,) + values.shape[1:])


def shards(node_state, node_dest, seg_nodes, seg_conn, pair_seg, pair_slot):
    dom_count = lax.axis_size(DOM)
    grp_count = lax.axis_size("grp")
    block_count = node_state.shape[0]
    capacity = max(2, 2 * block_count // dom_count)
    slot_count = dom_count * capacity
    order_ids = jnp.arange(block_count, dtype=jnp.int32)
    earlier = order_ids[None, :] < order_ids[:, None]
    same_dom = node_dest[:, None] == node_dest[None, :]
    slot_rank = jnp.sum((same_dom & earlier).astype(jnp.int32), axis=1)
    target_slot = node_dest * capacity + slot_rank
    outgoing = place_rows(target_slot, node_state, slot_count)
    received = two_step_exchange(outgoing, (("dom_0", "dom_1"), "dom_2"), (1, 0), 0, 0)
    corners = jnp.take(seg_nodes, seg_conn, axis=1)
    geometry = seg_geometry(corners)
    seg_blocks = geometry.shape[1] // SEG_BLK
    geo_blocks = jnp.transpose(geometry.reshape(9, seg_blocks, SEG_BLK), (1, 0, 2))
    seg_table = pair_seg[0]
    slot_table = pair_slot[0]
    geo_all = lax.all_gather(geo_blocks, "grp", axis=0, tiled=True)
    seg_in, slot_in = (
        lax.all_to_all(seg_table, "grp", split_axis=0, concat_axis=0, tiled=True),
        lax.all_to_all(slot_table, "grp", split_axis=0, concat_axis=0, tiled=True),
    )
    owner_base = (jnp.arange(grp_count, dtype=jnp.int32) * seg_blocks)[:, None]
    seg_ids = (seg_in + owner_base).reshape(-1)
    slot_ids = slot_in.reshape(-1)
    forces = jax.vmap(tile_force)(
        jnp.take(received, slot_ids, axis=0), jnp.take(geo_all, seg_ids, axis=0)
    )
    own_forces = place_rows(slot_ids, forces, slot_count)
    returned = lax.all_to_all(own_forces, DOM, split_axis=0, concat_axis=0, tiled=True)
    return jnp.take(returned, target_slot, axis=0)


def solution(mesh):
    split = Mesh(
        mesh.devices.reshape(mesh.shape["grp"], 16, 4, 2), ("grp", "dom_0", "dom_1", "dom_2")
    )
    placed = (
        P(GRP_DOM, None, None),
        P(GRP_DOM),
        P(None, GRP_DOM),
        P(None, GRP_DOM),
        P(GRP_DOM, None, None),
        P(GRP_DOM, None, None),
    )
    return jax.shard_map(
        shards, mesh=split, in_specs=placed, out_specs=P(GRP_DOM, None, None), check_vma=False
    )
```

profile of v0, /device:TPU:33, one launch (start us, length us, event | category | flops | bytes accessed | tf_op | source)
XLA Modules:
  0.0 168.8 jit_solution(1052670801400604042)
XLA Ops:
  0.0 0.9 convert_reduce_fusion
  0.9 0.7 compare_and_fusion.3
  1.6 1.2 copy.65
  2.7 0.0 copy-start
  2.8 0.5 fusion.34
  3.3 4.7 %all_to_all.39 = f32[64,2,2,6,128]{4,0,3,2,1:T(8,128)S(1)} all-to-all(f32[64,2,2,6,128]{4,0,3,2,1:T(8,128)S(1)} %fusion.34), channel_id=1, replica_groups=mesh['grp'=4,'dom_0'=16,'dom_1'=4,'dom_2'=2] {'dom_2'}, dimensions={1} | all-to-all | bytes 1572864 | tf_op jit(solution)/shard_map/all_to_all | solution.py:31
  8.0 4.0 %all-to-all-start.1 = ((s32[4,1,32]{2,1,0:T(1,128)}), s32[4,1,32]{2,1,0:T(1,128)S(1)}, u32[]{:S(2)}, u32[]{:S(2)}) async-start(s32[4,1,32]{2,1,0:T(1,128)} %bitcast.4), calls=%async_computation.1 | async-start | bytes 4096 | tf_op jit(solution)/shard_map/all_to_all | solution.py:105
  12.0 0.0 copy-done
  12.0 4.0 %all-to-all-done.1 = s32[4,1,32]{2,1,0:T(1,128)S(1)} async-done(((s32[4,1,32]{2,1,0:T(1,128)}), s32[4,1,32]{2,1,0:T(1,128)S(1)}, u32[]{:S(2)}, u32[]{:S(2)}) %all-to-all-start.1) | async-done | bytes 544 | tf_op jit(solution)/shard_map/all_to_all | solution.py:105
  16.0 3.2 %all-to-all-start = ((s32[4,1,32]{2,1,0:T(1,128)}), s32[4,1,32]{2,1,0:T(1,128)S(1)}, u32[]{:S(2)}, u32[]{:S(2)}) async-start(s32[4,1,32]{2,1,0:T(1,128)} %bitcast.1), calls=%async_computation | async-start | bytes 4096 | tf_op jit(solution)/shard_map/all_to_all | solution.py:106
  19.3 0.0 copy-start.1
  19.3 1.5 copy.66
  20.8 2.5 %all-to-all-done = s32[4,1,32]{2,1,0:T(1,128)S(1)} async-done(((s32[4,1,32]{2,1,0:T(1,128)}), s32[4,1,32]{2,1,0:T(1,128)S(1)}, u32[]{:S(2)}, u32[]{:S(2)}) %all-to-all-start) | async-done | bytes 544 | tf_op jit(solution)/shard_map/all_to_all | solution.py:106
  23.3 17.8 %all-to-all-start.3 = ((f32[64,2,2,6,128]{4,2,3,1,0:T(2,128)}), f32[64,2,2,6,128]{4,2,3,1,0:T(2,128)S(1)}, u32[]{:S(2)}, u32[]{:S(2)}) async-start(f32[64,2,2,6,128]{4,2,3,1,0:T(2,128)} %copy.66), calls=%async_computation.3 | async-start | bytes 1572864 | tf_op jit(solution)/shard_map/all_to_all | solution.py:31
  41.1 0.1 add.137
  41.2 0.1 add.148
  41.3 0.1 add.138
  41.4 0.0 copy-done.1
  41.4 0.1 copy.62
  41.5 8.1 %gather_fusion = f32[3072,6]{1,0:T(8,128)S(1)} fusion(f32[6,512]{0,1:T(8,128)S(1)} %copy.62, s32[3072]{0:T(1024)S(1)} %broadcast_clamp_fusion), kind=kCustom, calls=%fused_computation | custom fusion | bytes 159744 | tf_op jit(solution)/shard_map/jit(_take)/gather | solution.py:97
  49.6 0.5 copy.63
  50.3 9.9 %all_gather.3 = f32[32,9,128]{2,0,1:T(8,128)S(1)} all-gather(f32[8,9,128]{2,0,1:T(8,128)S(1)} %maximum_bitcast_fusion), channel_id=1, replica_groups=mesh['grp'=4,'dom_0'=16,'dom_1'=4,'dom_2'=2] {'grp'}, dimensions={0}, use_global_device_ids=true | all-gather | bytes 184320 | tf_op jit(solution)/shard_map/all_gather | solution.py:103
  60.1 0.1 copy.64
  60.2 0.1 all_to_all.30
  60.3 0.5 broadcast.150
  60.8 0.7 reduce.10
  61.5 0.1 all_to_all.29
  61.6 0.1 reshape.189
  61.7 0.7 reduce.11
  62.3 0.1 eq.61
  62.4 0.8 gather_fusion.1
  63.3 0.2 broadcast_select_fusion
  63.5 0.4 fusion.54
  63.9 16.5 %all-to-all-done.3 = f32[64,2,2,6,128]{4,2,3,1,0:T(2,128)S(1)} async-done(((f32[64,2,2,6,128]{4,2,3,1,0:T(2,128)}), f32[64,2,2,6,128]{4,2,3,1,0:T(2,128)S(1)}, u32[]{:S(2)}, u32[]{:S(2)}) %all-to-all-start.3) | async-done | bytes 786464 | tf_op jit(solution)/shard_map/all_to_all | solution.py:31
  80.4 0.3 copy.67
  80.7 0.5 copy.68
  81.1 0.8 gather_fusion.2
  81.9 0.2 broadcast_select_fusion.1
  82.1 0.3 fusion.55
  82.4 37.2 %fusion.14 = f32[128,3,128]{2,1,0:T(4,128)S(1)} fusion(f32[128,128]{1,0:T(8,128)S(1)} %bitcast.77, f32[128,128]{1,0:T(8,128)S(1)} %bitcast.86, f32[128,128]{1,0:T(8,128)S(1)} %bitcast.78, f32[128,128]{1,0:T(8,128)S(1)} %bitcast.79, f32[128,128]{1,0:T(8,128)S(1)} %bitcast.87, f32[128,128]{1,0:T(8,128)S(1)} %bitcast.80, f32[128,128]{1,0:T(8,128)S(1)} %bitcast.81, ...), kind=kOutput, calls=%fused_computation.24 | convolution fusion | flops 134217728 | bytes 1441792 | tf_op jit(solution)/shard_map/vmap()/dot_general | solution.py:68
  119.6 0.1 copy.69
  119.8 0.3 fusion.37
  120.1 1.1 copy.70
  121.2 12.2 %all-to-all-start.4 = ((f32[256,3,128]{2,1,0:T(4,128)}), f32[256,3,128]{2,1,0:T(4,128)S(1)}, u32[]{:S(2)}, u32[]{:S(2)}) async-start(f32[256,3,128]{2,1,0:T(4,128)} %copy.70), calls=%async_computation.4 | async-start | bytes 1048576 | tf_op jit(solution)/shard_map/all_to_all | solution.py:115
  133.5 33.7 %all-to-all-done.4 = f32[256,3,128]{2,1,0:T(4,128)S(1)} async-done(((f32[256,3,128]{2,1,0:T(4,128)}), f32[256,3,128]{2,1,0:T(4,128)S(1)}, u32[]{:S(2)}, u32[]{:S(2)}) %all-to-all-start.4) | async-done | bytes 393248 | tf_op jit(solution)/shard_map/all_to_all | solution.py:115
  167.1 0.8 gather_fusion.3
  167.9 0.2 broadcast_select_fusion.2
  168.1 0.7 copy.71
  (20 shorter events, 0.2 us)
Async XLA Ops:
  2.7 9.2 %copy-start = (s32[3,1024]{1,0:T(4,128)S(1)}, s32[3,1024]{1,0:T(4,128)}, u32[]{:S(2)}) copy-start(s32[3,1024]{1,0:T(4,128)} %param.9) | copy-start | bytes 36868
  8.0 8.1 %all-to-all-start.1 = ((s32[4,1,32]{2,1,0:T(1,128)}), s32[4,1,32]{2,1,0:T(1,128)S(1)}, u32[]{:S(2)}, u32[]{:S(2)}) async-start(s32[4,1,32]{2,1,0:T(1,128)} %bitcast.4), calls=%async_computation.1 | async-start | bytes 4096 | tf_op jit(solution)/shard_map/all_to_all | solution.py:105
  16.0 7.3 %all-to-all-start = ((s32[4,1,32]{2,1,0:T(1,128)}), s32[4,1,32]{2,1,0:T(1,128)S(1)}, u32[]{:S(2)}, u32[]{:S(2)}) async-start(s32[4,1,32]{2,1,0:T(1,128)} %bitcast.1), calls=%async_computation | async-start | bytes 4096 | tf_op jit(solution)/shard_map/all_to_all | solution.py:106
  19.3 22.1 %copy-start.1 = (f32[6,512]{1,0:T(8,128)S(1)}, f32[6,512]{1,0:T(8,128)}, u32[]{:S(2)}) copy-start(f32[6,512]{1,0:T(8,128)} %param.8) | copy-start | bytes 36868
  23.3 57.1 %all-to-all-start.3 = ((f32[64,2,2,6,128]{4,2,3,1,0:T(2,128)}), f32[64,2,2,6,128]{4,2,3,1,0:T(2,128)S(1)}, u32[]{:S(2)}, u32[]{:S(2)}) async-start(f32[64,2,2,6,128]{4,2,3,1,0:T(2,128)} %copy.66), calls=%async_computation.3 | async-start | bytes 1572864 | tf_op jit(solution)/shard_map/all_to_all | solution.py:31
  121.2 46.0 %all-to-all-start.4 = ((f32[256,3,128]{2,1,0:T(4,128)}), f32[256,3,128]{2,1,0:T(4,128)S(1)}, u32[]{:S(2)}, u32[]{:S(2)}) async-start(f32[256,3,128]{2,1,0:T(4,128)} %copy.70), calls=%async_computation.4 | async-start | bytes 1048576 | tf_op jit(solution)/shard_map/all_to_all | solution.py:115
where the time goes:
time: 169 us
  waiting for transfers between devices  56.7 us (34%)
  matrix products  38.1 us (23%)
  starting transfers between devices  37.3 us (22%)
  local copies, waits for them, and re-layouts  18.2 us (11%)
  blocking collectives  14.5 us (9%)
  other arithmetic  3.67 us (2%)
    dot_general x1, matrix products, tile_force(): jnp.dot(geometry[0:3], pressure, precision=lax.Precision.HIGHEST, preferr...  37.2 us
    all_to_all x1, waiting for transfers between devices, shards(): lax.all_to_all(own_forces, DOM, split_axis=0, concat_axis=0, tiled=True)  33.7 us
    all_to_all x1, starting transfers between devices, moved_by_axis(): lax.all_to_all(blocks, axes[k], split_axis=k, concat_axis=k, tiled=True)  17.8 us
    all_to_all x1, waiting for transfers between devices, moved_by_axis(): lax.all_to_all(blocks, axes[k], split_axis=k, concat_axis=k, tiled=True)  16.5 us
    all_to_all x1, starting transfers between devices, shards(): lax.all_to_all(own_forces, DOM, split_axis=0, concat_axis=0, tiled=True)  12.2 us
    all_gather x1, blocking collectives, shards(): geo_all = lax.all_gather(geo_blocks, 'grp', axis=0, tiled=True)  9.87 us
    gather x2, local copies, waits for them, and re-layouts, shards(): corners = jnp.take(seg_nodes, seg_conn, axis=1)  8.59 us
    all_to_all x1, blocking collectives, moved_by_axis(): lax.all_to_all(blocks, axes[k], split_axis=k, concat_axis=k, tiled=True)  4.67 us
  transfers between devices with their start and end apart: 4, of which 4 were waited for; matrix products, arithmetic and copies ran while one was open for 8% of the time, Pallas kernels for 0%

commit v1 on v0

--- a/solution.py
+++ b/solution.py
@@ -10,6 +10,28 @@
 time_step = 0.5
 stiffness = 0.5
 radius_sq = 0.5
+
+
+def cut_along(shard, dim, size):
+    before, after = (shard.shape[:dim], shard.shape[dim + 1 :])
+    return jnp.moveaxis(shard.reshape(*before, size, -1, *after), dim, 0)
+
+
+def laid_out(pieces, dim):
+    pieces = jnp.moveaxis(pieces, 0, dim)
+    shape = pieces.shape
+    return pieces.reshape(*shape[:dim], shape[dim] * shape[dim + 1], *shape[dim + 2 :])
+
+
+def rotated_exchange(x, axis, split_dim, concat_dim):
+    devices, index = (lax.axis_size(axis), lax.axis_index(axis))
+    tiles = cut_along(x, split_dim, devices)
+    outs = [tiles[index]]
+    for step in range(1, devices):
+        sent = tiles[(index + step) % devices]
+        outs.append(lax.ppermute(sent, axis, [(i, (i + step) % devices) for i in range(devices)]))
+    tiles = jnp.stack(outs)[(index - jnp.arange(devices)) % devices]
+    return laid_out(tiles, concat_dim)
 
 
 def in_blocks(shard, dim, devices):
@@ -102,7 +124,7 @@
     slot_table = pair_slot[0]
     geo_all = lax.all_gather(geo_blocks, "grp", axis=0, tiled=True)
     seg_in, slot_in = (
-        lax.all_to_all(seg_table, "grp", split_axis=0, concat_axis=0, tiled=True),
+        rotated_exchange(seg_table, "grp", 0, 0),
         lax.all_to_all(slot_table, "grp", split_axis=0, concat_axis=0, tiled=True),
     )
     owner_base = (jnp.arange(grp_count, dtype=jnp.int32) * seg_blocks)[:, None]

time: 169 us -> 175 us (1.036)
  starting transfers between devices: 37.3 us -> 41.5 us
  waiting for transfers between devices: 56.7 us -> 54.3 us
    ppermute x0 -> x3, starting transfers between devices: none -> 10.1 us  [rotated_exchange(): lax.ppermute(sent, axis, [(i, (i + step) % devices) for i in range(device...]
    all_to_all x1, waiting for transfers between devices: 16.5 us -> 20.6 us  [moved_by_axis(): lax.all_to_all(blocks, axes[k], split_axis=k, concat_axis=k, tiled=True)]
    all_to_all x1 -> x0, waiting for transfers between devices: 4.03 us -> none  [shards(): lax.all_to_all(seg_table, 'grp', split_axis=0, concat_axis=0, tiled=True)]
    all_to_all x1 -> x0, starting transfers between devices: 4.01 us -> none  [shards(): lax.all_to_all(seg_table, 'grp', split_axis=0, concat_axis=0, tiled=True)]
    all_to_all x1, starting transfers between devices: 12.2 us -> 9.48 us  [shards(): lax.all_to_all(own_forces, DOM, split_axis=0, concat_axis=0, tiled=True)]
    all_to_all x1, waiting for transfers between devices: 2.51 us -> 0.01 us  [shards(): lax.all_to_all(slot_table, 'grp', split_axis=0, concat_axis=0, tiled=True)]
  transfers between devices with their start and end apart: 4 -> 6, of which waited for: 4 -> 2; matrix products, arithmetic and copies ran while one was open for 8% -> 11% of each run, Pallas kernels for 0% -> 0%
where the time goes in v1:
time: 175 us; the launch traced here: 174 us
  waiting for transfers between devices  54.3 us (31%)
  starting transfers between devices  41.5 us (24%)
  matrix products  38.1 us (22%)
  local copies, waits for them, and re-layouts  19.3 us (11%)
  blocking collectives  16.1 us (9%)
  other arithmetic  4.53 us (3%)
    dot_general x1, matrix products, tile_force(): jnp.dot(geometry[0:3], pressure, precision=lax.Precision.HIGHEST, preferr...  37.2 us
    all_to_all x1, waiting for transfers between devices, shards(): lax.all_to_all(own_forces, DOM, split_axis=0, concat_axis=0, tiled=True)  33.7 us
    all_to_all x1, waiting for transfers between devices, moved_by_axis(): lax.all_to_all(blocks, axes[k], split_axis=k, concat_axis=k, tiled=True)  20.6 us
    all_to_all x1, starting transfers between devices, moved_by_axis(): lax.all_to_all(blocks, axes[k], split_axis=k, concat_axis=k, tiled=True)  17.8 us
    ppermute x3, starting transfers between devices, rotated_exchange(): lax.ppermute(sent, axis, [(i, (i + step) % devices) for i in range(device...  10.1 us
    all_gather x1, blocking collectives, shards(): geo_all = lax.all_gather(geo_blocks, 'grp', axis=0, tiled=True)  10 us
    all_to_all x1, starting transfers between devices, shards(): lax.all_to_all(own_forces, DOM, split_axis=0, concat_axis=0, tiled=True)  9.48 us
    gather x2, local copies, waits for them, and re-layouts, shards(): corners = jnp.take(seg_nodes, seg_conn, axis=1)  8.6 us
  transfers between devices with their start and end apart: 6, of which 2 were waited for; matrix products, arithmetic and copies ran while one was open for 11% of the time, Pallas kernels for 0%

profile of v1, /device:TPU:33, one launch (start us, length us, event | category | flops | bytes accessed | tf_op | source)
XLA Modules:
  0.0 174.2 jit_solution(1197932957835070772)
XLA Ops:
  0.0 4.0 %all-to-all-start = ((s32[4,1,32]{2,1,0:T(1,128)}), s32[4,1,32]{2,1,0:T(1,128)S(1)}, u32[]{:S(2)}, u32[]{:S(2)}) async-start(s32[4,1,32]{2,1,0:T(1,128)} %bitcast.104), calls=%async_computation | async-start | bytes 4096 | tf_op jit(solution)/shard_map/all_to_all | solution.py:128
  4.0 0.8 constant_dynamic-slice_fusion.3
  4.8 3.4 %collective-permute-start = (s32[1,32]{1,0:T(1,128)S(1)}, s32[1,32]{1,0:T(1,128)S(1)}, u32[]{:S(2)}, u32[]{:S(2)}) collective-permute-start(s32[1,32]{1,0:T(1,128)S(1)} %get-tuple-element.30), channel_id=1, source_target_pairs={{0,128},{128,256},{256,384},{384,0},{1,129},{129,257},{257,385},{3... | collective-permute-start | bytes 392 | tf_op jit(solution)/shard_map/ppermute | solution.py:32
  8.2 3.1 %collective-permute-start.2 = (s32[1,32]{1,0:T(1,128)S(1)}, s32[1,32]{1,0:T(1,128)S(1)}, u32[]{:S(2)}, u32[]{:S(2)}) collective-permute-start(s32[1,32]{1,0:T(1,128)S(1)} %get-tuple-element.31), channel_id=1, source_target_pairs={{0,384},{128,0},{256,128},{384,256},{1,385},{129,1},{257,129},{385... | collective-permute-start | bytes 392 | tf_op jit(solution)/shard_map/ppermute | solution.py:32
  11.4 3.7 %collective-permute-start.1 = (s32[1,32]{1,0:T(1,128)S(1)}, s32[1,32]{1,0:T(1,128)S(1)}, u32[]{:S(2)}, u32[]{:S(2)}) collective-permute-start(s32[1,32]{1,0:T(1,128)S(1)} %get-tuple-element.32), channel_id=1, source_target_pairs={{0,256},{128,384},{256,0},{384,128},{1,257},{129,385},{257,1},{385... | collective-permute-start | bytes 392 | tf_op jit(solution)/shard_map/ppermute | solution.py:32
  15.0 0.7 compare_and_fusion
  15.8 0.7 compare_select_fusion
  16.5 0.9 convert_reduce_fusion
  17.4 1.2 copy.62
  18.6 0.0 all-to-all-done
  18.6 0.5 broadcast.217
  19.1 0.7 reduce.5
  19.8 0.1 eq.67
  19.9 0.7 compare_and_fusion.3
  20.6 0.5 fusion.34
  21.1 6.1 %all_to_all.24 = f32[64,2,2,6,128]{4,0,3,2,1:T(8,128)S(1)} all-to-all(f32[64,2,2,6,128]{4,0,3,2,1:T(8,128)S(1)} %fusion.34), channel_id=1, replica_groups=mesh['grp'=4,'dom_0'=16,'dom_1'=4,'dom_2'=2] {'dom_2'}, dimensions={1} | all-to-all | bytes 1572864 | tf_op jit(solution)/shard_map/all_to_all | solution.py:53
  27.1 1.5 copy.63
  28.6 17.8 %all-to-all-start.2 = ((f32[64,2,2,6,128]{4,2,3,1,0:T(2,128)}), f32[64,2,2,6,128]{4,2,3,1,0:T(2,128)S(1)}, u32[]{:S(2)}, u32[]{:S(2)}) async-start(f32[64,2,2,6,128]{4,2,3,1,0:T(2,128)} %copy.63), calls=%async_computation.2 | async-start | bytes 1572864 | tf_op jit(solution)/shard_map/all_to_all | solution.py:53
  46.5 0.1 copy.59
  46.6 8.1 %gather_fusion.1 = f32[3072,6]{1,0:T(8,128)S(1)} fusion(f32[6,512]{0,1:T(8,128)S(1)} %copy.59, s32[3072]{0:T(1024)S(1)} %broadcast_clamp_fusion), kind=kCustom, calls=%fused_computation.1 | custom fusion | bytes 159744 | tf_op jit(solution)/shard_map/jit(_take)/gather | solution.py:119
  54.8 0.5 copy.60
  55.4 10.0 %all_gather.3 = f32[32,9,128]{2,0,1:T(8,128)S(1)} all-gather(f32[8,9,128]{2,0,1:T(8,128)S(1)} %maximum_bitcast_fusion), channel_id=1, replica_groups=mesh['grp'=4,'dom_0'=16,'dom_1'=4,'dom_2'=2] {'grp'}, dimensions={0}, use_global_device_ids=true | all-gather | bytes 184320 | tf_op jit(solution)/shard_map/all_gather | solution.py:125
  65.4 0.1 copy.61
  65.5 0.0 collective-permute-done.2
  65.5 0.0 collective-permute-done.1
  65.6 0.6 gather_fusion
  66.1 0.1 broadcast_add_fusion
  66.2 0.1 reshape.299
  66.3 0.1 reshape.298
  66.4 0.8 gather_fusion.2
  67.2 0.2 broadcast_select_fusion
  67.4 0.4 fusion.59
  67.8 0.1 reshape.249
  67.9 20.6 %all-to-all-done.2 = f32[64,2,2,6,128]{4,2,3,1,0:T(2,128)S(1)} async-done(((f32[64,2,2,6,128]{4,2,3,1,0:T(2,128)}), f32[64,2,2,6,128]{4,2,3,1,0:T(2,128)S(1)}, u32[]{:S(2)}, u32[]{:S(2)}) %all-to-all-start.2) | async-done | bytes 786464 | tf_op jit(solution)/shard_map/all_to_all | solution.py:53
  88.5 0.3 copy.64
  88.8 0.5 copy.65
  89.3 0.8 gather_fusion.3
  90.0 0.2 broadcast_select_fusion.1
  90.2 0.3 fusion.60
  90.5 37.2 %fusion.14 = f32[128,3,128]{2,1,0:T(4,128)S(1)} fusion(f32[128,128]{1,0:T(8,128)S(1)} %bitcast.86, f32[128,128]{1,0:T(8,128)S(1)} %bitcast.95, f32[128,128]{1,0:T(8,128)S(1)} %bitcast.87, f32[128,128]{1,0:T(8,128)S(1)} %bitcast.88, f32[128,128]{1,0:T(8,128)S(1)} %bitcast.96, f32[128,128]{1,0:T(8,128)S(1)} %bitcast.89, f32[128,128]{1,0:T(8,128)S(1)} %bitcast.90, ...), kind=kOutput, calls=%fused_computation.25 | convolution fusion | flops 134217728 | bytes 1441792 | tf_op jit(solution)/shard_map/vmap()/dot_general | solution.py:90
  127.7 0.1 copy.66
  127.9 0.3 fusion.37
  128.2 1.1 copy.67
  129.3 9.5 %all-to-all-start.3 = ((f32[256,3,128]{2,1,0:T(4,128)}), f32[256,3,128]{2,1,0:T(4,128)S(1)}, u32[]{:S(2)}, u32[]{:S(2)}) async-start(f32[256,3,128]{2,1,0:T(4,128)} %copy.67), calls=%async_computation.3 | async-start | bytes 1048576 | tf_op jit(solution)/shard_map/all_to_all | solution.py:137
  138.8 33.7 %all-to-all-done.3 = f32[256,3,128]{2,1,0:T(4,128)S(1)} async-done(((f32[256,3,128]{2,1,0:T(4,128)}), f32[256,3,128]{2,1,0:T(4,128)S(1)}, u32[]{:S(2)}, u32[]{:S(2)}) %all-to-all-start.3) | async-done | bytes 393248 | tf_op jit(solution)/shard_map/all_to_all | solution.py:137
  172.5 0.8 gather_fusion.4
  173.2 0.2 broadcast_select_fusion.2
  173.5 0.7 copy.68
  (23 shorter events, 0.2 us)
Async XLA Ops:
  0.0 18.6 %all-to-all-start = ((s32[4,1,32]{2,1,0:T(1,128)}), s32[4,1,32]{2,1,0:T(1,128)S(1)}, u32[]{:S(2)}, u32[]{:S(2)}) async-start(s32[4,1,32]{2,1,0:T(1,128)} %bitcast.104), calls=%async_computation | async-start | bytes 4096 | tf_op jit(solution)/shard_map/all_to_all | solution.py:128
  4.8 60.7 %collective-permute-start = (s32[1,32]{1,0:T(1,128)S(1)}, s32[1,32]{1,0:T(1,128)S(1)}, u32[]{:S(2)}, u32[]{:S(2)}) collective-permute-start(s32[1,32]{1,0:T(1,128)S(1)} %get-tuple-element.30), channel_id=1, source_target_pairs={{0,128},{128,256},{256,384},{384,0},{1,129},{129,257},{257,385},{3... | collective-permute-start | bytes 392 | tf_op jit(solution)/shard_map/ppermute | solution.py:32
  8.2 57.3 %collective-permute-start.2 = (s32[1,32]{1,0:T(1,128)S(1)}, s32[1,32]{1,0:T(1,128)S(1)}, u32[]{:S(2)}, u32[]{:S(2)}) collective-permute-start(s32[1,32]{1,0:T(1,128)S(1)} %get-tuple-element.31), channel_id=1, source_target_pairs={{0,384},{128,0},{256,128},{384,256},{1,385},{129,1},{257,129},{385... | collective-permute-start | bytes 392 | tf_op jit(solution)/shard_map/ppermute | solution.py:32
  11.4 54.2 %collective-permute-start.1 = (s32[1,32]{1,0:T(1,128)S(1)}, s32[1,32]{1,0:T(1,128)S(1)}, u32[]{:S(2)}, u32[]{:S(2)}) collective-permute-start(s32[1,32]{1,0:T(1,128)S(1)} %get-tuple-element.32), channel_id=1, source_target_pairs={{0,256},{128,384},{256,0},{384,128},{1,257},{129,385},{257,1},{385... | collective-permute-start | bytes 392 | tf_op jit(solution)/shard_map/ppermute | solution.py:32
  27.1 19.4 %copy-start = (f32[6,512]{1,0:T(8,128)S(1)}, f32[6,512]{1,0:T(8,128)}, u32[]{:S(2)}) copy-start(f32[6,512]{1,0:T(8,128)} %param.8) | copy-start | bytes 36868
  28.6 59.9 %all-to-all-start.2 = ((f32[64,2,2,6,128]{4,2,3,1,0:T(2,128)}), f32[64,2,2,6,128]{4,2,3,1,0:T(2,128)S(1)}, u32[]{:S(2)}, u32[]{:S(2)}) async-start(f32[64,2,2,6,128]{4,2,3,1,0:T(2,128)} %copy.63), calls=%async_computation.2 | async-start | bytes 1572864 | tf_op jit(solution)/shard_map/all_to_all | solution.py:53
  129.3 43.2 %all-to-all-start.3 = ((f32[256,3,128]{2,1,0:T(4,128)}), f32[256,3,128]{2,1,0:T(4,128)S(1)}, u32[]{:S(2)}, u32[]{:S(2)}) async-start(f32[256,3,128]{2,1,0:T(4,128)} %copy.67), calls=%async_computation.3 | async-start | bytes 1048576 | tf_op jit(solution)/shard_map/all_to_all | solution.py:137
